TPU v7x, 8 devices: a whole 2x2x1 slice. The times are simulated.
8 devices in a mesh: pod: 1 (over z), dp: 2 (over y), sp: 4 (over x, core).
Axes of the slice: x: 2, y: 2, z: 1, core: 2. Of those that a mesh axis runs over, the one named last changes fastest.
Arguments:
- x: bfloat16 [6, 192, 128, 1152], P(('pod', 'dp'), 'sp')
- norm_gain: bfloat16 [2, 2, 1152], replicated
- norm_shift: bfloat16 [2, 2, 1152], replicated
- w_qkv: bfloat16 [2, 3, 1152, 16, 72], replicated
- w_out: bfloat16 [2, 16, 72, 1152], replicated
- w_up: bfloat16 [2, 1152, 4608], replicated
- w_down: bfloat16 [2, 4608, 1152], replicated
Outputs:
- output: bfloat16 [6, 192, 128, 1152], P(('pod', 'dp'), 'sp')
All inputs are finite; a program needn't handle non-finite values.
Results may differ from a plain program's by a relative error of at most 0.0150801.
Values are sent between devices in bfloat16 or wider.
A program may use at most 1 GiB of HBM per device.

v0:
```python
import jax
import jax.numpy as jnp
from jax import lax
from jax.sharding import PartitionSpec as P

LN_EPS = 1e-6
SPATIAL_SCORE = 'btshe,btrhe->bthsr'
SPATIAL_MIX = 'bthsr,btrhe->btshe'
TEMPORAL_SCORE = 'btshe,bushe->bshtu'
TEMPORAL_MIX = 'bshtu,bushe->btshe'


def layer_norm(tokens, gain, shift):
    tok_f = tokens.astype(jnp.float32)
    mean_val = jnp.mean(tok_f, axis=-1, keepdims=True)
    centered = tok_f - mean_val
    var_val = jnp.mean(centered * centered, axis=-1, keepdims=True)
    normed = centered * lax.rsqrt(var_val + LN_EPS)
    return (normed * gain.astype(jnp.float32) + shift.astype(jnp.float32)).astype(jnp.bfloat16)


def attn_inputs(tokens, gains, shifts, w_qkv):
    normed = layer_norm(tokens, gains[0], shifts[0])
    return jnp.einsum('btsd,kdhe->kbtshe', normed, w_qkv, preferred_element_type=jnp.float32).astype(jnp.bfloat16)


def attn_core(proj_qkv, score_form, mix_form):
    head_dim = proj_qkv.shape[-1]
    scores = jnp.einsum(score_form, proj_qkv[0], proj_qkv[1], preferred_element_type=jnp.float32) * (head_dim ** -0.5)
    attn_probs = jax.nn.softmax(scores, axis=-1).astype(jnp.bfloat16)
    return jnp.einsum(mix_form, attn_probs, proj_qkv[2], preferred_element_type=jnp.float32).astype(jnp.bfloat16)


def block_tail(tokens, mixed, gains, shifts, w_out, w_up, w_down):
    attn_proj = jnp.einsum('btshe,hed->btsd', mixed, w_out, preferred_element_type=jnp.float32).astype(jnp.bfloat16)
    hidden = (tokens.astype(jnp.float32) + attn_proj.astype(jnp.float32)).astype(jnp.bfloat16)
    normed_mlp = layer_norm(hidden, gains[1], shifts[1])
    up_proj = jnp.dot(normed_mlp, w_up, preferred_element_type=jnp.float32).astype(jnp.bfloat16)
    activated = jax.nn.gelu(up_proj.astype(jnp.float32), approximate=True).astype(jnp.bfloat16)
    down_proj = jnp.dot(activated, w_down, preferred_element_type=jnp.float32).astype(jnp.bfloat16)
    return (hidden.astype(jnp.float32) + down_proj.astype(jnp.float32)).astype(jnp.bfloat16)


def value_a9(tokens, gains, shifts, w_qkv, w_out, w_up, w_down, score_form, mix_form):
    mixed = attn_core(attn_inputs(tokens, gains, shifts, w_qkv), score_form, mix_form)
    return block_tail(tokens, mixed, gains, shifts, w_out, w_up, w_down)


def solution(mesh):
    tok_spec = P(('pod', 'dp'), 'sp', None, None)

    def local_step(x_loc, norm_gain, norm_shift, w_qkv, w_out, w_up, w_down):
        spatial_out = value_a9(x_loc, norm_gain[0], norm_shift[0], w_qkv[0], w_out[0], w_up[0], w_down[0], SPATIAL_SCORE, SPATIAL_MIX)
        by_patch = lax.all_to_all(spatial_out, 'sp', 2, 1, tiled=True)
        temporal_out = value_a9(by_patch, norm_gain[1], norm_shift[1], w_qkv[1], w_out[1], w_up[1], w_down[1], TEMPORAL_SCORE, TEMPORAL_MIX)
        return lax.all_to_all(temporal_out, 'sp', 1, 2, tiled=True)

    return jax.shard_map(local_step, mesh=mesh, in_specs=(tok_spec, P(), P(), P(), P(), P(), P()), out_specs=tok_spec, check_vma=False)
```

profile of v0, /device:TPU:0, one launch (start us, length us, event | category | flops | bytes accessed | tf_op | source)
XLA Modules:
  0.0 4256.1 jit_solution(8235891998758732906)
XLA Ops:
  0.0 0.0 copy-start.1
  0.0 0.0 copy-start
  0.0 13.7 convert_reduce_fusion.2
  13.8 17.1 fusion.40
  30.9 0.0 copy-done.1
  30.9 0.0 copy-done
  30.9 0.7 convert_reduce_fusion.3
  31.6 186.6 %convert_bitcast_fusion.1 = bf16[3,3,48,128,16,72]{3,5,4,0,2,1:T(8,128)(2,1)} fusion(bf16[3,48,128,1152]{3,2,1,0:T(8,128)(2,1)} %param.7, f32[1152]{0:T(1024)S(1)} %get-tuple-element.11, f32[1152]{0:T(1024)S(1)} %get-tuple-element.25, f32[3,48,128]{2,1,0:T(8,128)S(1)} %add_rsqrt_fusion.3, f32[3,48,128]{2,1,0:T(8,128)S(1)} %broadcast_multiply_fusion.3, ...), kind=kOutput, calls=%fused_computation.41 | convolution fusion | flops 146958188544 | bytes 177988608 | tf_op jit(solution)/shard_map/btsd,kdhe->kbtshe/dot_general | solution.py:24
  218.2 80.5 %fusion.62 = f32[3,48,16,128,128]{3,4,2,1,0:T(8,128)} fusion(bf16[3,3,48,128,16,72]{3,5,4,0,2,1:T(8,128)(2,1)} %convert_bitcast_fusion.1), kind=kOutput, calls=%fused_computation.89 | convolution fusion | flops 5435817984 | bytes 235929600 | tf_op jit(solution)/shard_map/btshe,btrhe->bthsr/dot_general | solution.py:29
  298.7 145.2 %fusion.117 = (f32[3,48,16,128]{3,2,1,0:T(8,128)}, f32[3,48,16,128,128]{3,4,2,1,0:T(8,128)}) fusion(f32[3,48,16,128,128]{3,4,2,1,0:T(8,128)} %fusion.62), kind=kOutput, calls=%fused_computation.148 | output fusion | flops 150995072 | bytes 303169536 | tf_op jit(solution)/shard_map/sub | solution.py:30
  443.9 2.0 fusion.104.clone.5
  445.9 0.0 copy-start.6
  445.9 0.0 copy-start.7
  445.9 102.1 %convert_reduce_fusion.1 = (f32[3,48,128]{2,1,0:T(8,128)S(1)}, bf16[3,48,128,1152]{3,2,1,0:T(8,128)(2,1)}) fusion(f32[3,48,16,128,128]{3,4,2,1,0:T(8,128)} %get-tuple-element.17, f32[3,48,16,128]{3,2,1,0:T(8,128)} %get-tuple-element.16, bf16[3,3,48,128,16,72]{3,5,4,0,2,1:T(8,128)(2,1)} %convert_bitcast_fusion.1, bf16[3,48,128,1152]{3,2,1,0:T(8,128)(2,1)} %param.7, ...), kind=kOutput, calls=%fused_computation.40 | convolution fusion | flops 54603530240 | bytes 282304512 | tf_op jit(solution)/shard_map/btshe,hed->btsd/dot_general | solution.py:35
  548.1 17.1 fusion.36
  565.2 0.0 copy-done.6
  565.2 0.0 copy-done.7
  565.2 235.8 %fusion.58 = bf16[3,48,128,4608]{3,2,1,0:T(8,128)(2,1)} fusion(bf16[3,48,128,1152]{3,2,1,0:T(8,128)(2,1)} %get-tuple-element.19, f32[1152]{0:T(1024)S(1)} %copy-done.6, f32[1152]{0:T(1024)S(1)} %copy-done.7, f32[3,48,128]{2,1,0:T(8,128)S(1)} %add_rsqrt_fusion.2, f32[3,48,128]{2,1,0:T(8,128)S(1)} %broadcast_multiply_fusion.2, bf16[2,1152,4608]{2,1,0:T(8,128)(2,1)} %param.12), kind=kOutput, calls=%fused_computation.86 | convolution fusion | flops 195816849408 | bytes 223110144 | tf_op jit(solution)/shard_map/dot_general | solution.py:38
  801.0 261.8 %fusion.45 = bf16[3,48,128,1152]{3,2,1,0:T(8,128)(2,1)} fusion(bf16[3,48,128,1152]{3,2,1,0:T(8,128)(2,1)} %get-tuple-element.19, bf16[3,48,128,4608]{3,2,1,0:T(8,128)(2,1)} %fusion.58, bf16[2,4608,1152]{2,1,0:T(8,128)(2,1)} %param.13), kind=kOutput, calls=%fused_computation.64 | convolution fusion | flops 196644962304 | bytes 265420800 | tf_op jit(solution)/shard_map/dot_general | solution.py:40
  1062.8 28.5 copy.13
  1091.3 11.7 all-to-all-start
  1103.0 7.1 fusion.154
  1110.0 451.9 %all-to-all-done = bf16[3,48,128,1152]{3,1,0,2:T(8,128)(2,1)} async-done(((bf16[3,48,128,1152]{3,1,0,2:T(8,128)(2,1)}), bf16[3,48,128,1152]{3,1,0,2:T(8,128)(2,1)}, u32[]{:S(2)}, u32[]{:S(2)}) %all-to-all-start) | async-done | bytes 42467360 | tf_op jit(solution)/shard_map/all_to_all | solution.py:54
  1561.9 41.9 bitcast_convert_fusion.2
  1603.8 0.0 copy-start.2
  1603.8 0.0 copy-start.3
  1603.8 38.3 bitcast_reduce_fusion
  1642.1 38.8 multiply_reduce_fusion.2
  1680.9 0.0 copy-done.2
  1680.9 0.0 copy-done.3
  1681.0 42.1 add_convert_fusion.1
  1723.0 306.5 %convert_bitcast_fusion = bf16[3,3,192,32,16,72]{5,3,4,0,2,1:T(8,128)(2,1)} fusion(bf16[3,192,32,1152,1,1]{3,2,5,4,1,0:T(8,128)(2,1)} %bitcast.186, bf16[3,1152,16,72,1,1]{1,3,2,0,5,4:T(8,128)(2,1)} %fusion.154), kind=kOutput, calls=%fused_computation.26 | convolution fusion | flops 146830786560 | bytes 177831936 | tf_op jit(solution)/shard_map/btsd,kdhe->kbtshe/dot_general | solution.py:24
  2029.5 147.2 %slice_bitcast_fusion.2 = (bf16[3,192,32,16,72]{4,2,3,1,0:T(8,128)(2,1)}, bf16[3,192,32,16,72]{4,2,3,1,0:T(8,128)(2,1)}, bf16[3,192,32,16,72]{4,2,3,1,0:T(8,128)(2,1)}) fusion(bf16[3,3,192,32,16,72]{5,3,4,0,2,1:T(8,128)(2,1)} %convert_bitcast_fusion), kind=kLoop, calls=%fused_computation.75 | loop fusion | bytes 254803968 | tf_op jit(solution)/shard_map/squeeze | solution.py:31
  2176.7 331.3 %fusion.50 = f32[3,32,16,192,192]{3,4,2,1,0:T(8,128)} fusion(bf16[3,192,32,16,72]{4,2,3,1,0:T(8,128)(2,1)} %get-tuple-element.14, bf16[3,192,32,16,72]{4,2,3,1,0:T(8,128)(2,1)} %get-tuple-element.15), kind=kOutput, calls=%fused_computation.79 | convolution fusion | flops 8153726976 | bytes 311427072 | tf_op jit(solution)/shard_map/btshe,bushe->bshtu/dot_general | solution.py:29
  2508.1 286.0 %fusion.118 = (f32[3,32,16,192]{3,2,1,0:T(8,128)S(1)}, f32[3,32,16,192,192]{3,4,2,1,0:T(8,128)}) fusion(f32[3,32,16,192,192]{3,4,2,1,0:T(8,128)} %fusion.50), kind=kOutput, calls=%fused_computation.149 | output fusion | flops 226492608 | bytes 454164480 | tf_op jit(solution)/shard_map/sub | solution.py:30
  2794.0 169.2 %fusion.22 = bf16[3,32,16,72,192]{4,3,2,1,0:T(8,128)(2,1)} fusion(f32[3,32,16,192,192]{3,4,2,1,0:T(8,128)} %get-tuple-element.21, f32[3,32,16,192]{3,2,1,0:T(8,128)S(1)} %get-tuple-element.20, bf16[3,192,32,16,72]{4,2,3,1,0:T(8,128)(2,1)} %get-tuple-element.13), kind=kOutput, calls=%fused_computation.32 | convolution fusion | flops 8266973184 | bytes 312606720 | tf_op jit(solution)/shard_map/bshtu,bushe->btshe/dot_general | solution.py:31
  2963.2 97.8 %copy.28 = bf16[3,32,16,72,192]{3,1,2,4,0:T(8,128)(2,1)} copy(bf16[3,32,16,72,192]{4,3,2,1,0:T(8,128)(2,1)} %fusion.22) | data formatting | bytes 84934656 | tf_op jit(solution)/shard_map/bshtu,bushe->btshe/dot_general | solution.py:31
  3061.0 41.5 copy.14
  3102.6 0.0 copy-start.4
  3102.6 79.8 %convert_reduce_fusion = (f32[3,192,32]{2,1,0:T(8,128)S(1)}, bf16[3,192,32,1152]{3,2,1,0:T(8,128)(2,1)}) fusion(f32[3,192,32,1152]{3,2,1,0:T(8,128)} %bitcast.23, bf16[2,16,72,1152]{3,2,1,0:T(8,128)(2,1)} %param.11, bf16[3,32,16,72,192]{3,1,2,4,0:T(8,128)(2,1)} %copy.28), kind=kOutput, calls=%fused_computation.37 | convolution fusion | flops 49049747456 | bytes 205627392 | tf_op jit(solution)/shard_map/btshe,hed->btsd/dot_general | solution.py:35
  3182.4 19.7 fusion.32
  3202.2 0.0 copy-done.4
  3202.2 0.0 copy-done.5
  3202.2 283.0 %fusion.159 = bf16[3,192,32,4608]{3,2,1,0:T(8,128)(2,1)} fusion(bf16[3,192,32,1152]{3,2,1,0:T(8,128)(2,1)} %get-tuple-element.23, f32[1152]{0:T(1024)S(1)} %copy-done.4, f32[1152]{0:T(1024)S(1)} %copy-done.5, f32[3,192,32]{2,1,0:T(8,128)S(1)} %add_rsqrt_fusion, f32[3,192,32]{2,1,0:T(8,128)S(1)} %broadcast_multiply_fusion, ...), kind=kOutput, calls=%fused_computation.21.clone.clone.clone.clone.2 | convolution fusion | flops 196751130624 | bytes 223110144 | tf_op jit(solution)/shard_map/dot_general | solution.py:38
  3485.2 233.2 %fusion.46 = bf16[3,192,32,1152]{3,2,1,0:T(8,128)(2,1)} fusion(bf16[3,192,32,1152]{3,2,1,0:T(8,128)(2,1)} %get-tuple-element.23, bf16[2,4608,1152]{2,1,0:T(8,128)(2,1)} %param.13, bf16[3,192,32,4608]{3,2,1,0:T(8,128)(2,1)} %fusion.159), kind=kOutput, calls=%fused_computation.65 | convolution fusion | flops 195795615744 | bytes 265420800 | tf_op jit(solution)/shard_map/dot_general | solution.py:40
  3718.4 28.6 copy.17
  3747.0 479.9 %all_to_all.27 = bf16[3,192,32,1152]{3,2,0,1:T(8,128)(2,1)} all-to-all(bf16[3,192,32,1152]{3,2,0,1:T(8,128)(2,1)} %copy.17), channel_id=1, replica_groups=mesh['pod'=1,'dp'=2,'sp'=4] {'sp'}, dimensions={1} | all-to-all | bytes 84934656 | tf_op jit(solution)/shard_map/all_to_all | solution.py:56
  4227.0 28.7 copy.18
  (9 shorter events, 0.2 us)
Async XLA Ops:
  0.0 30.9 copy-start.1
  0.0 30.9 copy-start
  445.9 119.3 %copy-start.6 = (f32[1152]{0:T(1024)S(1)}, f32[1152]{0:T(1024)}, u32[]{:S(2)}) copy-start(f32[1152]{0:T(1024)} %get-tuple-element.10) | copy-start | bytes 13828
  445.9 119.3 %copy-start.7 = (f32[1152]{0:T(1024)S(1)}, f32[1152]{0:T(1024)}, u32[]{:S(2)}) copy-start(f32[1152]{0:T(1024)} %get-tuple-element.26) | copy-start | bytes 13828
  1091.3 470.7 %all-to-all-start = ((bf16[3,48,128,1152]{3,1,0,2:T(8,128)(2,1)}), bf16[3,48,128,1152]{3,1,0,2:T(8,128)(2,1)}, u32[]{:S(2)}, u32[]{:S(2)}) async-start(bf16[3,48,128,1152]{3,1,0,2:T(8,128)(2,1)} %copy.13), calls=%async_computation | async-start | bytes 84934656 | tf_op jit(solution)/shard_map/all_to_all | solution.py:54
  1603.8 77.1 %copy-start.2 = (f32[1152]{0:T(1024)S(1)}, f32[1152]{0:T(1024)}, u32[]{:S(2)}) copy-start(f32[1152]{0:T(1024)} %get-tuple-element.12) | copy-start | bytes 13828
  1603.8 77.1 %copy-start.3 = (f32[1152]{0:T(1024)S(1)}, f32[1152]{0:T(1024)}, u32[]{:S(2)}) copy-start(f32[1152]{0:T(1024)} %get-tuple-element.24) | copy-start | bytes 13828
  3102.6 99.6 %copy-start.4 = (f32[1152]{0:T(1024)S(1)}, f32[1152]{0:T(1024)}, u32[]{:S(2)}) copy-start(f32[1152]{0:T(1024)} %get-tuple-element.9) | copy-start | bytes 13828
  3102.6 99.6 %copy-start.5 = (f32[1152]{0:T(1024)S(1)}, f32[1152]{0:T(1024)}, u32[]{:S(2)}) copy-start(f32[1152]{0:T(1024)} %get-tuple-element.27) | copy-start | bytes 13828
where the time goes:
time: 4270 us; the launch traced here: 4260 us
  matrix products  2270 us (53%)
  other arithmetic  661 us (15%)
  blocking collectives  480 us (11%)
  waiting for transfers between devices  452 us (11%)
  local copies, waits for them, and re-layouts  381 us (9%)
    dot_general x2, matrix products, block_tail(): jnp.dot(normed_mlp, w_up, preferred_element_type=jnp.float32)  519 us
    dot_general x2, matrix products, block_tail(): jnp.dot(activated, w_down, preferred_element_type=jnp.float32)  495 us
    dot_general x2, matrix products, attn_inputs(): jnp.einsum('btsd,kdhe->kbtshe', normed, w_qkv, preferred_element_type=jnp...  493 us
    all_to_all x1, blocking collectives, local_step(): return lax.all_to_all(temporal_out, 'sp', 1, 2, tiled=True)  480 us
    all_to_all x1, waiting for transfers between devices, local_step(): by_patch = lax.all_to_all(spatial_out, 'sp', 2, 1, tiled=True)  452 us
    sub x2, other arithmetic, attn_core(): attn_probs = jax.nn.softmax(scores, axis=-1).astype(jnp.bfloat16)  431 us
    dot_general x2, matrix products, attn_core(): jnp.einsum(score_form, proj_qkv[0], proj_qkv[1], preferred_element_type=j...  412 us
    dot_general x2, matrix products, block_tail(): jnp.einsum('btshe,hed->btsd', mixed, w_out, preferred_element_type=jnp.fl...  182 us
  transfers between devices with their start and end apart: 1, of which 1 were waited for; matrix products, arithmetic and copies ran while one was open for 0% of the time, Pallas kernels for 0%

commit v1 on v0

v1 whole, which is shorter than its diff:
```python
import functools
import math

import jax
import jax.numpy as jnp
from jax import lax
from jax.experimental import pallas as pl
from jax.experimental.pallas import tpu as pltpu
from jax.sharding import PartitionSpec as P

LN_EPS = 1e-6
HEADS = 16
HEAD = 72
ROWS = 80
WIDTH = HEADS * HEAD
WIDE = HEADS * ROWS
FF = 4 * WIDTH
SPATIAL_HEADS, TEMPORAL_HEADS = 8, 8
SOFTMAX_SCALE = (HEAD ** -0.5) * math.log2(math.e)
VMEM_LIMIT = 60 * 1024 * 1024
F32 = jnp.float32
BF16 = jnp.bfloat16


def layer_norm(tokens, gain, shift):
    tok = tokens.astype(F32)
    centered = tok - jnp.mean(tok, axis=-1, keepdims=True)
    var = jnp.mean(centered * centered, axis=-1, keepdims=True)
    normed = centered * lax.rsqrt(var + LN_EPS)
    return (normed * gain.astype(F32) + shift.astype(F32)).astype(BF16)


def project_qkv(n_s, w_ref, qkv_s, length, stride):
    for j in range(3):
        rows = pl.ds(j * WIDE, WIDE)
        proj = lax.dot_general(
            w_ref[rows, :], n_s[...], (((1,), (1,)), ((), ())), preferred_element_type=F32
        ).astype(BF16)
        if length == stride:
            qkv_s[rows, :] = proj
        else:
            for p in range(proj.shape[1] // length):
                qkv_s[rows, pl.ds(p * stride, length)] = proj[:, p * length:(p + 1) * length]


def attend_all(qkv_s, o_s, sequences, length, stride, heads):
    def refs(head, seq):
        row = pl.multiple_of(head * ROWS, 16)
        return row, pl.ds(seq * stride, length)

    def per_step(step, carry):
        units = [(step * heads + i, seq) for i in range(heads) for seq in range(sequences)]
        scores = []
        for head, seq in units:
            row, cols = refs(head, seq)
            q = qkv_s[pl.ds(row, ROWS), cols]
            k = qkv_s[pl.ds(WIDE + row, ROWS), cols]
            scores.append(lax.dot_general(k, q, (((0,), (0,)), ((), ())), preferred_element_type=F32))
        probs = []
        for s in scores:
            e = jnp.exp2((s - jnp.max(s, axis=0, keepdims=True)) * SOFTMAX_SCALE)
            probs.append((e * (1.0 / jnp.sum(e, axis=0, keepdims=True))).astype(BF16))
        for (head, seq), p in zip(units, probs):
            row, cols = refs(head, seq)
            v = qkv_s[pl.ds(2 * WIDE + row, ROWS), cols]
            o = jnp.dot(v, p, preferred_element_type=F32)
            o_s[pl.ds(row, ROWS), pl.ds(seq * length, length)] = o.astype(BF16)
        return carry

    lax.fori_loop(0, HEADS // heads, per_step, 0)


def project_out(o_s, w_ref):
    return lax.dot_general(o_s[...], w_ref[...], (((0,), (0,)), ((), ())), preferred_element_type=F32).astype(BF16)


def spatial_kernel(x_ref, gain_ref, shift_ref, wqkv_ref, wout_ref, h_ref, n_s, qkv_s, o_s):
    frames, patches, width = h_ref.shape
    tok = frames * patches
    n_s[...] = layer_norm(x_ref[0].reshape(tok, width), gain_ref[...], shift_ref[...])
    project_qkv(n_s, wqkv_ref, qkv_s, patches, patches)

    attend_all(qkv_s, o_s, frames, patches, patches, SPATIAL_HEADS)
    a = project_out(o_s, wout_ref)
    h = x_ref[0].reshape(tok, width).astype(F32) + a.astype(F32)
    h_ref[...] = h.astype(BF16).reshape(frames, patches, width)


def temporal_kernel(stride, x_ref, gain_ref, shift_ref, wqkv_ref, wout_ref, h_ref, n_s, qkv_s, o_s, a_s):
    groups, patches, frames, width = x_ref.shape
    length = groups * frames
    for p in range(patches):
        for g in range(groups):
            n_s[pl.ds(p * length + g * frames, frames), :] = layer_norm(x_ref[g, p], gain_ref[...], shift_ref[...])
    project_qkv(n_s, wqkv_ref, qkv_s, length, stride)

    attend_all(qkv_s, o_s, patches, length, stride, TEMPORAL_HEADS)
    a_s[...] = project_out(o_s, wout_ref)
    for p in range(patches):
        for g in range(groups):
            a = a_s[pl.ds(p * length + g * frames, frames), :]
            h_ref[g, p] = (x_ref[g, p].astype(F32) + a.astype(F32)).astype(BF16)


def mlp_kernel(chunk, h_ref, gain_ref, shift_ref, up_ref, down_ref, *rest):
    y_ref, n_s, acc_s = rest[-3:]
    h = h_ref[...]
    n_s[...] = layer_norm(h, gain_ref[...], shift_ref[...])
    for c in range(0, FF, chunk):
        u = jnp.dot(n_s[...], up_ref[:, c:c + chunk], preferred_element_type=F32).astype(BF16)
        g = jax.nn.gelu(u.astype(F32), approximate=True).astype(BF16)
        part = jnp.dot(g, down_ref[c:c + chunk, :], preferred_element_type=F32)
        if c == 0:
            acc_s[...] = part
        elif c + chunk < FF:
            acc_s[...] += part
        else:
            m = (acc_s[...] + part).astype(BF16)
            y_ref[...] = (h.astype(F32) + m.astype(F32)).astype(BF16).reshape(y_ref.shape)


def pick(array, *at):
    rest = array.shape[len(at):]
    return pl.BlockSpec((None,) * len(at) + rest, lambda i: at + (0,) * len(rest), pipeline_mode=pl.Buffered(1))


def params():
    return pltpu.CompilerParams(dimension_semantics=("arbitrary",), vmem_limit_bytes=VMEM_LIMIT)


def attention_cost(tokens, keys):
    return pl.CostEstimate(
        flops=2 * tokens * WIDTH * (4 * WIDTH + 2 * keys), bytes_accessed=4 * tokens * WIDTH, transcendentals=tokens * keys * HEADS
    )


def spatial_attention(x, video, gain, shift, wqkv, wout, frames=4):
    _, num_frames, patches, width = x.shape
    tok = frames * patches
    return pl.pallas_call(
        spatial_kernel,
        name="spatial_attention",
        grid=(num_frames // frames,),
        in_specs=[
            pl.BlockSpec((1, frames, patches, width), lambda i: (video, i, 0, 0)),
            pick(gain, 0, 0), pick(shift, 0, 0), pick(wqkv, 0), pick(wout, 0),
        ],
        out_specs=pl.BlockSpec((frames, patches, width), lambda i: (i, 0, 0)),
        out_shape=jax.ShapeDtypeStruct((num_frames, patches, width), BF16),
        scratch_shapes=[
            pltpu.VMEM((tok, width), BF16), pltpu.VMEM((3 * WIDE, tok), BF16), pltpu.VMEM((WIDE, tok), BF16),
        ],
        compiler_params=params(),
        cost_estimate=attention_cost(num_frames * patches, patches),
    )(x, gain, shift, wqkv, wout)


def temporal_attention(x, gain, shift, wqkv, wout, patches=4):
    groups, num_patches, frames, width = x.shape
    length = groups * frames
    stride = -(-length // 128) * 128
    tok = patches * length
    spec = pl.BlockSpec((groups, patches, frames, width), lambda i: (0, i, 0, 0))
    return pl.pallas_call(
        functools.partial(temporal_kernel, stride),
        name="temporal_attention",
        grid=(num_patches // patches,),
        in_specs=[spec, pick(gain, 1, 0), pick(shift, 1, 0), pick(wqkv, 1), pick(wout, 1)],
        out_specs=spec,
        out_shape=jax.ShapeDtypeStruct(x.shape, BF16),
        scratch_shapes=[
            pltpu.VMEM((tok, width), BF16), pltpu.VMEM((3 * WIDE, patches * stride), BF16), pltpu.VMEM((WIDE, tok), BF16),
            pltpu.VMEM((tok, width), BF16),
        ],
        compiler_params=params(),
        cost_estimate=attention_cost(num_patches * length, length),
    )(x, gain, shift, wqkv, wout)


def mlp(h, block, gain, shift, w_up, w_down, videos=None, video=0, into=None, tok=512, chunk=1536):
    tokens, width = h.shape
    in_specs = [
        pl.BlockSpec((tok, width), lambda i: (i, 0)),
        pick(gain, block, 1), pick(shift, block, 1), pick(w_up, block), pick(w_down, block),
    ]
    args = [h, gain, shift, w_up, w_down]
    aliases = {}
    if videos is None:
        out_spec = pl.BlockSpec((tok, width), lambda i: (i, 0))
        out_shape = jax.ShapeDtypeStruct((tokens, width), BF16)
    else:
        out_spec = pl.BlockSpec((1, tok, width), lambda i: (video, i, 0))
        out_shape = jax.ShapeDtypeStruct((videos, tokens, width), BF16)
    if into is not None:
        in_specs.append(pl.BlockSpec(memory_space=pl.ANY))
        args.append(into)
        aliases = {len(args) - 1: 0}
    return pl.pallas_call(
        functools.partial(mlp_kernel, chunk),
        name="mlp",
        grid=(tokens // tok,),
        in_specs=in_specs,
        out_specs=out_spec,
        out_shape=out_shape,
        scratch_shapes=[pltpu.VMEM((tok, width), BF16), pltpu.VMEM((tok, width), F32)],
        input_output_aliases=aliases,
        compiler_params=params(),
        cost_estimate=pl.CostEstimate(
            flops=4 * tokens * width * FF, bytes_accessed=4 * tokens * width + 4 * width * FF, transcendentals=tokens * FF
        ),
    )(*args)


def pad_heads(w_qkv, w_out):
    pad = ROWS - HEAD
    wqkv = jnp.pad(jnp.transpose(w_qkv, (0, 1, 3, 4, 2)), ((0, 0), (0, 0), (0, 0), (0, pad), (0, 0)))
    wout = jnp.pad(w_out, ((0, 0), (0, 0), (0, pad), (0, 0)))
    return wqkv.reshape(-1, 3 * WIDE, WIDTH), wout.reshape(-1, WIDE, WIDTH)


def solution(mesh):
    tok_spec = P(('pod', 'dp'), 'sp', None, None)
    sp = mesh.shape['sp']

    def local_step(x, norm_gain, norm_shift, w_qkv, w_out, w_up, w_down):
        videos, frames, patches, width = x.shape
        gain, shift = norm_gain[:, :, None, :], norm_shift[:, :, None, :]
        wqkv, wout = pad_heads(w_qkv, w_out)

        sent = []
        for v in range(videos):
            h = spatial_attention(x, v, gain, shift, wqkv, wout)
            t = mlp(h.reshape(frames * patches, width), 0, gain, shift, w_up, w_down)
            t = jnp.transpose(t.reshape(frames, patches, width), (1, 0, 2)).reshape(sp, patches // sp, frames, width)
            sent.append(lax.all_to_all(t, 'sp', 0, 0, tiled=True))
        back = []
        for v in range(videos):
            h = temporal_attention(sent[v], gain, shift, wqkv, wout)
            back.append(lax.all_to_all(h, 'sp', 0, 0, tiled=True))
        y = None
        for v in range(videos):
            if v:
                back[v], y = lax.optimization_barrier((back[v], y))
            h = jnp.transpose(back[v].reshape(patches, frames, width), (1, 0, 2)).reshape(frames * patches, width)
            y = mlp(h, 1, gain, shift, w_up, w_down, videos, v, y)
        return y.reshape(videos, frames, patches, width)

    return jax.shard_map(
        local_step, mesh=mesh, in_specs=(tok_spec, P(), P(), P(), P(), P(), P()), out_specs=tok_spec, check_vma=False
    )
```

time: 4270 us -> 2020 us (0.47)
  matrix products: 2270 us -> 0 us
  Pallas kernels: 0 us -> 1840 us
  other arithmetic: 661 us -> 0 us
  blocking collectives: 480 us -> 0 us
  waiting for transfers between devices: 452 us -> 19.9 us
  local copies, waits for them, and re-layouts: 381 us -> 104 us
    dot_general x11 -> x0, matrix products: 2270 us -> none  [the longest x2 519 us: block_tail(): jnp.dot(normed_mlp, w_up, preferred_element_type=jnp.float32)]
    pallas_call x0 -> x12, Pallas kernels: none -> 1840 us  [the longest x6 1060 us: mlp(): pl.pallas_call(functools.partial(mlp_kernel, chunk), name='mlp', grid=(to...]
    all_to_all x1 -> x0, blocking collectives: 480 us -> none  [local_step(): return lax.all_to_all(temporal_out, 'sp', 1, 2, tiled=True)]
    all_to_all x1 -> x6, waiting for transfers between devices: 452 us -> 19.9 us  [the longest x3 19.9 us: local_step(): sent.append(lax.all_to_all(t, 'sp', 0, 0, tiled=True))]
    sub x2 -> x0, other arithmetic: 431 us -> none  [attn_core(): attn_probs = jax.nn.softmax(scores, axis=-1).astype(jnp.bfloat16)]
    squeeze x1 -> x0, local copies, waits for them, and re-layouts: 147 us -> none  [attn_core(): proj_qkv[2]]
    reduce_sum x6 -> x0, other arithmetic: 145 us -> none  [the longest x4 92.7 us: layer_norm(): var_val = jnp.mean(centered * centered, axis=-1, keepdims=True)]
    dot_general x2 -> x0, local copies, waits for them, and re-layouts: 105 us -> none  [the longest x1 97.8 us: attn_core(): jnp.einsum(mix_form, attn_probs, proj_qkv[2], preferred_element_type=jnp....]
  transfers between devices with their start and end apart: 1 -> 6, of which waited for: 1 -> 1; matrix products, arithmetic and copies ran while one was open for 0% -> 3% of each run, Pallas kernels for 0% -> 68%
where the time goes in v1:
time: 2020 us; the launch traced here: 2010 us
  Pallas kernels  1840 us (91%)
  local copies, waits for them, and re-layouts  104 us (5%)
  starting transfers between devices  40 us (2%)
    pallas_call x6, Pallas kernels, mlp(): pl.pallas_call(functools.partial(mlp_kernel, chunk), name='mlp', grid=(to...  1060 us
    pallas_call x3, Pallas kernels, temporal_attention(): pl.pallas_call(functools.partial(temporal_kernel, stride), name='temporal...  409 us
    pallas_call x3, Pallas kernels, spatial_attention(): pl.pallas_call(spatial_kernel, name='spatial_attention', grid=(num_frames...  380 us
    reshape x3, local copies, waits for them, and re-layouts, local_step(): back[v].reshape(patches, frames, width)  48.1 us
  transfers between devices with their start and end apart: 6, of which 1 were waited for; matrix products, arithmetic and copies ran while one was open for 3% of the time, Pallas kernels for 68%

profile of v1, /device:TPU:0, one launch (start us, length us, event | category | flops | bytes accessed | tf_op | source)
XLA Modules:
  0.0 2009.1 jit_solution(16165989275065201091)
XLA Ops:
  0.0 1.3 copy.16.gain_ref
  1.3 1.3 copy.17.shift_ref
  2.6 5.5 pad.9
  8.1 12.4 pad.8
  20.5 126.8 %spatial_attention.5 = bf16[48,128,1152]{2,1,0:T(8,128)(2,1)} custom-call(bf16[3,48,128,1152]{3,2,1,0:T(8,128)(2,1)} %x_ref.5, bf16[2,2,1,1152]{3,2,1,0:T(2,128)(2,1)} %copy.16.gain_ref, bf16[2,2,1,1152]{3,2,1,0:T(2,128)(2,1)} %copy.17.shift_ref, bf16[2,3840,1152]{2,1,0:T(8,128)(2,1)} %bitcast.36, bf16[2,1280,1152]{2,1,0:T(8,128)(2,1)} %bitcast.49), custom_call_target="tpu_custom_call" | custom-call | flops 68853694464 | bytes 28311552 | tf_op jit(solution)/shard_map/spatial_attention/pallas_call | solution.py:140
  147.3 176.0 %mlp.8 = bf16[6144,1152]{1,0:T(8,128)(2,1)} custom-call(bf16[6144,1152]{1,0:T(8,128)(2,1)} %bitcast.58, bf16[2,2,1,1152]{3,2,1,0:T(2,128)(2,1)} %copy.16.gain_ref, bf16[2,2,1,1152]{3,2,1,0:T(2,128)(2,1)} %copy.17.shift_ref, bf16[2,1152,4608]{2,1,0:T(8,128)(2,1)} %up_ref.11, bf16[2,4608,1152]{2,1,0:T(8,128)(2,1)} %down_ref.11), custom_call_target="tpu_custom_call" | custom-call | flops 130459631616 | bytes 49545216 | tf_op jit(solution)/shard_map/mlp/pallas_call | solution.py:198
  323.3 11.8 copy.34
  335.1 6.5 all-to-all-start.4
  341.7 126.8 %spatial_attention.4 = bf16[48,128,1152]{2,1,0:T(8,128)(2,1)} custom-call(bf16[3,48,128,1152]{3,2,1,0:T(8,128)(2,1)} %x_ref.5, bf16[2,2,1,1152]{3,2,1,0:T(2,128)(2,1)} %copy.16.gain_ref, bf16[2,2,1,1152]{3,2,1,0:T(2,128)(2,1)} %copy.17.shift_ref, bf16[2,3840,1152]{2,1,0:T(8,128)(2,1)} %bitcast.37, bf16[2,1280,1152]{2,1,0:T(8,128)(2,1)} %bitcast.50), custom_call_target="tpu_custom_call" | custom-call | flops 68853694464 | bytes 28311552 | tf_op jit(solution)/shard_map/spatial_attention/pallas_call | solution.py:140
  468.5 176.3 %mlp.7 = bf16[6144,1152]{1,0:T(8,128)(2,1)} custom-call(bf16[6144,1152]{1,0:T(8,128)(2,1)} %bitcast.59, bf16[2,2,1,1152]{3,2,1,0:T(2,128)(2,1)} %copy.16.gain_ref, bf16[2,2,1,1152]{3,2,1,0:T(2,128)(2,1)} %copy.17.shift_ref, bf16[2,1152,4608]{2,1,0:T(8,128)(2,1)} %up_ref.11, bf16[2,4608,1152]{2,1,0:T(8,128)(2,1)} %down_ref.11), custom_call_target="tpu_custom_call" | custom-call | flops 130459631616 | bytes 49545216 | tf_op jit(solution)/shard_map/mlp/pallas_call | solution.py:198
  644.8 11.9 copy.27
  656.6 126.7 %spatial_attention.3 = bf16[48,128,1152]{2,1,0:T(8,128)(2,1)} custom-call(bf16[3,48,128,1152]{3,2,1,0:T(8,128)(2,1)} %x_ref.5, bf16[2,2,1,1152]{3,2,1,0:T(2,128)(2,1)} %copy.16.gain_ref, bf16[2,2,1,1152]{3,2,1,0:T(2,128)(2,1)} %copy.17.shift_ref, bf16[2,3840,1152]{2,1,0:T(8,128)(2,1)} %bitcast.38, bf16[2,1280,1152]{2,1,0:T(8,128)(2,1)} %bitcast.51), custom_call_target="tpu_custom_call" | custom-call | flops 68853694464 | bytes 28311552 | tf_op jit(solution)/shard_map/spatial_attention/pallas_call | solution.py:140
  783.3 0.0 all-to-all-done.4.x_ref
  783.3 6.8 all-to-all-start.2
  790.1 175.9 %mlp.6 = bf16[6144,1152]{1,0:T(8,128)(2,1)} custom-call(bf16[6144,1152]{1,0:T(8,128)(2,1)} %bitcast.57, bf16[2,2,1,1152]{3,2,1,0:T(2,128)(2,1)} %copy.16.gain_ref, bf16[2,2,1,1152]{3,2,1,0:T(2,128)(2,1)} %copy.17.shift_ref, bf16[2,1152,4608]{2,1,0:T(8,128)(2,1)} %up_ref.11, bf16[2,4608,1152]{2,1,0:T(8,128)(2,1)} %down_ref.11), custom_call_target="tpu_custom_call" | custom-call | flops 130459631616 | bytes 49545216 | tf_op jit(solution)/shard_map/mlp/pallas_call | solution.py:198
  966.0 12.0 copy.20
  978.0 0.0 all-to-all-done.2.x_ref
  978.0 6.5 all-to-all-start
  984.5 136.0 %temporal_attention.5 = bf16[4,32,48,1152]{3,2,1,0:T(8,128)(2,1)} custom-call(bf16[4,32,48,1152]{3,2,1,0:T(8,128)(2,1)} %all-to-all-done.4.x_ref, bf16[2,2,1,1152]{3,2,1,0:T(2,128)(2,1)} %copy.16.gain_ref, bf16[2,2,1,1152]{3,2,1,0:T(2,128)(2,1)} %copy.17.shift_ref, bf16[2,3840,1152]{2,1,0:T(8,128)(2,1)} %bitcast.39, bf16[2,1280,1152]{2,1,0:T(8,128)(2,1)} %bitcast.52), custom_call_target="tpu_custom_call" | custom-call | flops 70665633792 | bytes 28311552 | tf_op jit(solution)/shard_map/temporal_attention/pallas_call | solution.py:164
  1120.6 19.9 all-to-all-done.x_ref
  1140.5 6.8 all-to-all-start.5
  1147.2 136.1 %temporal_attention.4 = bf16[4,32,48,1152]{3,2,1,0:T(8,128)(2,1)} custom-call(bf16[4,32,48,1152]{3,2,1,0:T(8,128)(2,1)} %all-to-all-done.2.x_ref, bf16[2,2,1,1152]{3,2,1,0:T(2,128)(2,1)} %copy.16.gain_ref, bf16[2,2,1,1152]{3,2,1,0:T(2,128)(2,1)} %copy.17.shift_ref, bf16[2,3840,1152]{2,1,0:T(8,128)(2,1)} %bitcast.40, bf16[2,1280,1152]{2,1,0:T(8,128)(2,1)} %bitcast.53), custom_call_target="tpu_custom_call" | custom-call | flops 70665633792 | bytes 28311552 | tf_op jit(solution)/shard_map/temporal_attention/pallas_call | solution.py:164
  1283.4 136.4 %temporal_attention.3 = bf16[4,32,48,1152]{3,2,1,0:T(8,128)(2,1)} custom-call(bf16[4,32,48,1152]{3,2,1,0:T(8,128)(2,1)} %all-to-all-done.x_ref, bf16[2,2,1,1152]{3,2,1,0:T(2,128)(2,1)} %copy.16.gain_ref, bf16[2,2,1,1152]{3,2,1,0:T(2,128)(2,1)} %copy.17.shift_ref, bf16[2,3840,1152]{2,1,0:T(8,128)(2,1)} %bitcast.41, bf16[2,1280,1152]{2,1,0:T(8,128)(2,1)} %bitcast.54), custom_call_target="tpu_custom_call" | custom-call | flops 70665633792 | bytes 28311552 | tf_op jit(solution)/shard_map/temporal_attention/pallas_call | solution.py:164
  1419.8 0.0 all-to-all-done.5
  1419.8 6.6 all-to-all-start.3
  1426.4 16.0 copy.37
  1442.3 176.2 %mlp.9.rest_0_ = bf16[3,6144,1152]{2,1,0:T(8,128)(2,1)} custom-call(bf16[6144,1152]{1,0:T(8,128)(2,1)} %bitcast.48, bf16[2,2,1,1152]{3,2,1,0:T(2,128)(2,1)} %copy.16.gain_ref, bf16[2,2,1,1152]{3,2,1,0:T(2,128)(2,1)} %copy.17.shift_ref, bf16[2,1152,4608]{2,1,0:T(8,128)(2,1)} %up_ref.11, bf16[2,4608,1152]{2,1,0:T(8,128)(2,1)} %down_ref.11), custom_call_target="tpu_custom_call" | custom-call | flops 130459631616 | bytes 49545216 | tf_op jit(solution)/shard_map/mlp/pallas_call | solution.py:198
  1618.5 0.0 all-to-all-done.3
  1618.5 6.8 all-to-all-start.1
  1625.3 16.0 copy.40
  1641.3 175.7 %mlp.10.rest_0_ = bf16[3,6144,1152]{2,1,0:T(8,128)(2,1)} custom-call(bf16[6144,1152]{1,0:T(8,128)(2,1)} %bitcast.44, bf16[2,2,1,1152]{3,2,1,0:T(2,128)(2,1)} %copy.16.gain_ref, bf16[2,2,1,1152]{3,2,1,0:T(2,128)(2,1)} %copy.17.shift_ref, bf16[2,1152,4608]{2,1,0:T(8,128)(2,1)} %up_ref.11, ...), custom_call_target="tpu_custom_call", output_to_operand_aliasing={{}: (5, {})} | custom-call | flops 130459631616 | bytes 49545216 | tf_op jit(solution)/shard_map/mlp/pallas_call | solution.py:198
  1817.0 0.0 all-to-all-done.1
  1817.0 16.2 copy.43
  1833.2 175.7 %mlp.11 = bf16[3,6144,1152]{2,1,0:T(8,128)(2,1)} custom-call(bf16[6144,1152]{1,0:T(8,128)(2,1)} %bitcast.43, bf16[2,2,1,1152]{3,2,1,0:T(2,128)(2,1)} %copy.16.gain_ref, bf16[2,2,1,1152]{3,2,1,0:T(2,128)(2,1)} %copy.17.shift_ref, bf16[2,1152,4608]{2,1,0:T(8,128)(2,1)} %up_ref.11, bf16[2,4608,1152]{2,1,0:T(8,128)(2,1)} %down_ref.11, ...), custom_call_target="tpu_custom_call", output_to_operand_aliasing={{}: (5, {})} | custom-call | flops 130459631616 | bytes 49545216 | tf_op jit(solution)/shard_map/mlp/pallas_call | solution.py:198
Async XLA Ops:
  335.1 448.2 %all-to-all-start.4 = ((bf16[4,32,48,1152]{3,2,1,0:T(8,128)(2,1)}), bf16[4,32,48,1152]{3,2,1,0:T(8,128)(2,1)}, u32[]{:S(2)}, u32[]{:S(2)}) async-start(bf16[4,32,48,1152]{3,2,1,0:T(8,128)(2,1)} %bitcast.35), calls=%async_computation.4 | async-start | bytes 28311552 | tf_op jit(solution)/shard_map/all_to_all | solution.py:235
  783.3 194.7 %all-to-all-start.2 = ((bf16[4,32,48,1152]{3,2,1,0:T(8,128)(2,1)}), bf16[4,32,48,1152]{3,2,1,0:T(8,128)(2,1)}, u32[]{:S(2)}, u32[]{:S(2)}) async-start(bf16[4,32,48,1152]{3,2,1,0:T(8,128)(2,1)} %bitcast.33), calls=%async_computation.2 | async-start | bytes 28311552 | tf_op jit(solution)/shard_map/all_to_all | solution.py:235
  978.0 162.5 %all-to-all-start = ((bf16[4,32,48,1152]{3,2,1,0:T(8,128)(2,1)}), bf16[4,32,48,1152]{3,2,1,0:T(8,128)(2,1)}, u32[]{:S(2)}, u32[]{:S(2)}) async-start(bf16[4,32,48,1152]{3,2,1,0:T(8,128)(2,1)} %bitcast.34), calls=%async_computation | async-start | bytes 28311552 | tf_op jit(solution)/shard_map/all_to_all | solution.py:235
  1140.5 279.3 %all-to-all-start.5 = ((bf16[4,32,48,1152]{3,2,1,0:T(8,128)(2,1)}), bf16[4,32,48,1152]{3,2,1,0:T(8,128)(2,1)}, u32[]{:S(2)}, u32[]{:S(2)}) async-start(bf16[4,32,48,1152]{3,2,1,0:T(8,128)(2,1)} %temporal_attention.5), calls=%async_computation.5 | async-start | bytes 28311552 | tf_op jit(solution)/shard_map/all_to_all | solution.py:239
  1419.8 198.7 %all-to-all-start.3 = ((bf16[4,32,48,1152]{3,2,1,0:T(8,128)(2,1)}), bf16[4,32,48,1152]{3,2,1,0:T(8,128)(2,1)}, u32[]{:S(2)}, u32[]{:S(2)}) async-start(bf16[4,32,48,1152]{3,2,1,0:T(8,128)(2,1)} %temporal_attention.4), calls=%async_computation.3 | async-start | bytes 28311552 | tf_op jit(solution)/shard_map/all_to_all | solution.py:239
  1618.5 198.5 %all-to-all-start.1 = ((bf16[4,32,48,1152]{3,2,1,0:T(8,128)(2,1)}), bf16[4,32,48,1152]{3,2,1,0:T(8,128)(2,1)}, u32[]{:S(2)}, u32[]{:S(2)}) async-start(bf16[4,32,48,1152]{3,2,1,0:T(8,128)(2,1)} %temporal_attention.3), calls=%async_computation.1 | async-start | bytes 28311552 | tf_op jit(solution)/shard_map/all_to_all | solution.py:239
